TPU v7x, 32 devices: a whole 2x2x4 slice. The times are simulated.
32 devices in a mesh: rep: 4 (over x, y), pp: 8 (over z, core).
Axes of the slice: x: 2, y: 2, z: 4, core: 2. Of those that a mesh axis runs over, the one named last changes fastest.
Arguments:
- x: bfloat16 [64, 512, 512], P('rep'), parts along dimension 0
- dy: bfloat16 [64, 512, 512], P('rep'), parts along dimension 0
- w_gate: bfloat16 [8, 512, 1280], P('pp')
- w_up: bfloat16 [8, 512, 1280], P('pp')
- w_down: bfloat16 [8, 1280, 512], P('pp')
Outputs:
- output 1: bfloat16 [32, 512, 1280], P(('rep', 'pp')), parts along dimension 0
- output 2: bfloat16 [32, 512, 1280], P(('rep', 'pp')), parts along dimension 0
- output 3: bfloat16 [32, 1280, 512], P(('rep', 'pp')), parts along dimension 0
There are 4 independent parts. A program takes and returns all parts, laid end to end along the dimension named above; an argument that names none is the same for every part.
All inputs are finite; a program needn't handle non-finite values.
Results may differ from a plain program's by a relative error of at most 0.0266.
Values are sent between devices in bfloat16 or wider.
A program may use at most 2 GiB of HBM per device.

v0:
```python
import jax
import jax.numpy as jnp
from jax import lax
from jax.sharding import PartitionSpec as P

NAMES = ("w_gate", "w_up", "w_down")


def matmul(a, w):
    return jnp.dot(a, w, preferred_element_type=jnp.float32).astype(jnp.bfloat16)


def normed(h):
    wide = h.astype(jnp.float32)
    scale = lax.rsqrt(jnp.mean(wide**2, -1, keepdims=True) + 1e-6)
    return (wide * scale).astype(jnp.bfloat16)


def layer(h, w):
    a = normed(h)
    gate = jnp.dot(a, w["w_gate"], preferred_element_type=jnp.float32)
    up = jnp.dot(a, w["w_up"], preferred_element_type=jnp.float32)
    return h + matmul((jax.nn.silu(gate) * up).astype(jnp.bfloat16), w["w_down"])


def stage(weights, h):
    for number in range(weights["w_gate"].shape[0]):
        h = layer(h, {name: w[number] for name, w in weights.items()})
    return h


def solution(mesh):
    stages = mesh.shape["pp"]
    onward = [(i, i + 1) for i in range(stages - 1)]
    back_again = [(i + 1, i) for i in range(stages - 1)]

    def step(x, dy, *arrays):
        weights = dict(zip(NAMES, arrays, strict=True))
        micro, me = x.shape[0], lax.axis_index("pp")
        kept, came = jnp.zeros_like(x), jnp.zeros_like(x[0])
        for t in range(micro + stages - 1):
            number = jnp.clip(t - me, 0, micro - 1)
            at_work = (t >= me) & (t - me < micro)
            h = jnp.where(me == 0, x[min(t, micro - 1)], came)
            was = lax.dynamic_index_in_dim(kept, number, 0, keepdims=False)
            kept = lax.dynamic_update_index_in_dim(kept, jnp.where(at_work, h, was), number, 0)
            came = lax.ppermute(stage(weights, h), "pp", onward)
        total = {name: jnp.zeros(w.shape, jnp.float32) for name, w in weights.items()}
        came, behind = jnp.zeros_like(x[0]), stages - 1 - me
        for t in range(micro + stages - 1):
            number = jnp.clip(t - behind, 0, micro - 1)
            at_work = (t >= behind) & (t - behind < micro)
            by_y = jnp.where(behind == 0, dy[min(t, micro - 1)], came)
            _, back = jax.vjp(stage, weights, lax.dynamic_index_in_dim(kept, number, 0, keepdims=False))
            by_w, by_h = back(by_y)
            total = {name: total[name] + jnp.where(at_work, by_w[name].astype(jnp.float32), 0.0) for name in NAMES}
            came = lax.ppermute(by_h, "pp", back_again)
        return tuple(total[name].astype(jnp.bfloat16) for name in NAMES)

    return jax.shard_map(
        step,
        mesh=mesh,
        in_specs=(P("rep", None, None),) * 2 + (P("pp", None, None),) * 3,
        out_specs=(P(("rep", "pp"), None, None),) * 3,
        check_vma=False,
    )
```

profile of v0, /device:TPU:13, one launch (start us, length us, event | category | flops | bytes accessed | tf_op | source)
XLA Modules:
  0.0 1039.0 jit_solution(10890733391021317922)
XLA Ops:
  5.7 4.8 fusion.1035
  14.2 6.1 collective-permute-done
  24.0 4.9 fusion.1032
  33.3 6.1 collective-permute-done.1
  43.1 4.9 fusion.1029
  52.5 6.1 collective-permute-done.2
  63.0 5.2 fusion.1026
  72.6 6.1 collective-permute-done.3
  83.2 5.2 fusion.1023
  88.4 4.6 collective-permute-start.4
  93.0 5.9 collective-permute-done.4
  103.4 5.2 fusion.1020
  113.0 6.1 collective-permute-done.5
  123.5 5.2 fusion.1017
  133.1 6.1 collective-permute-done.6
  143.7 5.2 fusion.1014
  153.3 6.1 collective-permute-done.7
  163.8 5.2 fusion.1011
  173.4 6.1 collective-permute-done.8
  184.0 5.2 fusion.1008
  189.2 4.6 collective-permute-start.9
  193.8 5.8 collective-permute-done.9
  204.3 4.8 fusion.1005
  209.2 4.5 collective-permute-start.10
  227.3 4.8 fusion.1002
  244.9 4.8 fusion.999
  264.9 4.8 fusion.996
  269.8 4.9 collective-permute-start.13
  285.2 4.9 fusion.993
  305.0 4.8 fusion.990
  309.9 4.5 collective-permute-start.15
  325.1 4.8 fusion.987
  329.9 4.5 collective-permute-start.16
  345.2 4.8 fusion.984
  350.0 4.7 collective-permute-start.17
  365.2 4.8 fusion.981
  385.2 4.9 fusion.978
  390.1 4.5 collective-permute-start.19
  405.3 4.9 fusion.975
  410.2 4.5 collective-permute-start.20
  425.4 4.8 fusion.972
  430.2 4.7 collective-permute-start.21
  468.6 5.7 collective-permute-done.22
  514.5 5.9 collective-permute-done.24
  540.2 5.8 collective-permute-done.25
  565.8 5.9 collective-permute-done.26
  591.7 5.6 collective-permute-done.27
  616.9 6.0 collective-permute-done.28
  642.6 5.9 collective-permute-done.29
  668.3 5.8 collective-permute-done.30
  694.1 5.6 collective-permute-done.31
  719.4 5.9 collective-permute-done.32
  745.0 5.9 collective-permute-done.33
  770.7 5.8 collective-permute-done.34
  796.4 5.6 collective-permute-done.35
  821.8 5.9 collective-permute-done.36
  847.4 5.9 collective-permute-done.37
  873.1 5.8 collective-permute-done.38
  898.9 5.6 collective-permute-done.39
  924.2 5.9 collective-permute-done.40
  949.9 5.9 collective-permute-done.41
  975.5 5.8 collective-permute-done.42
  1001.2 5.7 collective-permute-done.43
  1021.7 16.8 %fusion.229 = bf16[1,1280,512]{2,1,0:T(8,128)(2,1)} fusion(f32[1280,512]{1,0:T(8,128)} %fusion.206, f32[1280,512]{1,0:T(8,128)} %fusion.204, f32[1280,512]{1,0:T(8,128)} %fusion.202, f32[1280,512]{1,0:T(8,128)} %fusion.200, f32[1280,512]{1,0:T(8,128)} %fusion.198, f32[1280,512]{1,0:T(8,128)} %fusion.196, f32[1280,512]{1,0:T(8,128)} %fusion.194, ...), kind=kOutput, calls=%fused_computation.412 | convolution fusion | flops 692060160 | bytes 64749568 | tf_op jit(solution)/shard_map/transpose(jvp())/dot_general | solution.py:10
  (542 shorter events, 681.2 us)
Async XLA Ops:
  10.4 9.8 collective-permute-start
  28.9 10.5 %collective-permute-start.1 = (bf16[512,512]{1,0:T(8,128)(2,1)}, bf16[512,512]{1,0:T(8,128)(2,1)S(1)}, u32[]{:S(2)}, u32[]{:S(2)}) collective-permute-start(bf16[512,512]{1,0:T(8,128)(2,1)} %fusion.1032), channel_id=1, source_target_pairs={{0,1},{1,2},{2,3},{3,4},{4,5},{5,6},{6,7},{8,9},{9,10},{10,11},{11... | collective-permute-start | bytes 1572872 | tf_op jit(solution)/shard_map/ppermute | solution.py:47
  48.0 10.5 %collective-permute-start.2 = (bf16[512,512]{1,0:T(8,128)(2,1)}, bf16[512,512]{1,0:T(8,128)(2,1)S(1)}, u32[]{:S(2)}, u32[]{:S(2)}) collective-permute-start(bf16[512,512]{1,0:T(8,128)(2,1)} %fusion.1029), channel_id=1, source_target_pairs={{0,1},{1,2},{2,3},{3,4},{4,5},{5,6},{6,7},{8,9},{9,10},{10,11},{11... | collective-permute-start | bytes 1572872 | tf_op jit(solution)/shard_map/ppermute | solution.py:47
  68.2 10.5 %collective-permute-start.3 = (bf16[512,512]{1,0:T(8,128)(2,1)}, bf16[512,512]{1,0:T(8,128)(2,1)S(1)}, u32[]{:S(2)}, u32[]{:S(2)}) collective-permute-start(bf16[512,512]{1,0:T(8,128)(2,1)} %fusion.1026), channel_id=1, source_target_pairs={{0,1},{1,2},{2,3},{3,4},{4,5},{5,6},{6,7},{8,9},{9,10},{10,11},{11... | collective-permute-start | bytes 1572872 | tf_op jit(solution)/shard_map/ppermute | solution.py:47
  88.4 10.5 %collective-permute-start.4 = (bf16[512,512]{1,0:T(8,128)(2,1)}, bf16[512,512]{1,0:T(8,128)(2,1)S(1)}, u32[]{:S(2)}, u32[]{:S(2)}) collective-permute-start(bf16[512,512]{1,0:T(8,128)(2,1)} %fusion.1023), channel_id=1, source_target_pairs={{0,1},{1,2},{2,3},{3,4},{4,5},{5,6},{6,7},{8,9},{9,10},{10,11},{11... | collective-permute-start | bytes 1572872 | tf_op jit(solution)/shard_map/ppermute | solution.py:47
  108.6 10.5 %collective-permute-start.5 = (bf16[512,512]{1,0:T(8,128)(2,1)}, bf16[512,512]{1,0:T(8,128)(2,1)S(1)}, u32[]{:S(2)}, u32[]{:S(2)}) collective-permute-start(bf16[512,512]{1,0:T(8,128)(2,1)} %fusion.1020), channel_id=1, source_target_pairs={{0,1},{1,2},{2,3},{3,4},{4,5},{5,6},{6,7},{8,9},{9,10},{10,11},{11... | collective-permute-start | bytes 1572872 | tf_op jit(solution)/shard_map/ppermute | solution.py:47
  128.7 10.5 %collective-permute-start.6 = (bf16[512,512]{1,0:T(8,128)(2,1)}, bf16[512,512]{1,0:T(8,128)(2,1)S(1)}, u32[]{:S(2)}, u32[]{:S(2)}) collective-permute-start(bf16[512,512]{1,0:T(8,128)(2,1)} %fusion.1017), channel_id=1, source_target_pairs={{0,1},{1,2},{2,3},{3,4},{4,5},{5,6},{6,7},{8,9},{9,10},{10,11},{11... | collective-permute-start | bytes 1572872 | tf_op jit(solution)/shard_map/ppermute | solution.py:47
  148.8 10.5 %collective-permute-start.7 = (bf16[512,512]{1,0:T(8,128)(2,1)}, bf16[512,512]{1,0:T(8,128)(2,1)S(1)}, u32[]{:S(2)}, u32[]{:S(2)}) collective-permute-start(bf16[512,512]{1,0:T(8,128)(2,1)} %fusion.1014), channel_id=1, source_target_pairs={{0,1},{1,2},{2,3},{3,4},{4,5},{5,6},{6,7},{8,9},{9,10},{10,11},{11... | collective-permute-start | bytes 1572872 | tf_op jit(solution)/shard_map/ppermute | solution.py:47
  169.0 10.5 %collective-permute-start.8 = (bf16[512,512]{1,0:T(8,128)(2,1)}, bf16[512,512]{1,0:T(8,128)(2,1)S(1)}, u32[]{:S(2)}, u32[]{:S(2)}) collective-permute-start(bf16[512,512]{1,0:T(8,128)(2,1)} %fusion.1011), channel_id=1, source_target_pairs={{0,1},{1,2},{2,3},{3,4},{4,5},{5,6},{6,7},{8,9},{9,10},{10,11},{11... | collective-permute-start | bytes 1572872 | tf_op jit(solution)/shard_map/ppermute | solution.py:47
  189.2 10.5 %collective-permute-start.9 = (bf16[512,512]{1,0:T(8,128)(2,1)}, bf16[512,512]{1,0:T(8,128)(2,1)}, u32[]{:S(2)}, u32[]{:S(2)}) collective-permute-start(bf16[512,512]{1,0:T(8,128)(2,1)} %fusion.1008), channel_id=1, source_target_pairs={{0,1},{1,2},{2,3},{3,4},{4,5},{5,6},{6,7},{8,9},{9,10},{10,11},{11... | collective-permute-start | bytes 1572872 | tf_op jit(solution)/shard_map/ppermute | solution.py:47
  209.2 10.5 %copy-start.51 = (bf16[1,1280,512]{2,1,0:T(8,128)(2,1)S(1)}, bf16[1,1280,512]{2,1,0:T(8,128)(2,1)}, u32[]{:S(2)}) copy-start(bf16[1,1280,512]{2,1,0:T(8,128)(2,1)} %param.9) | copy-start | bytes 3932164
  209.2 13.5 %collective-permute-start.10 = (bf16[512,512]{1,0:T(8,128)(2,1)}, bf16[512,512]{1,0:T(8,128)(2,1)S(1)}, u32[]{:S(2)}, u32[]{:S(2)}) collective-permute-start(bf16[512,512]{1,0:T(8,128)(2,1)} %fusion.1005), channel_id=1, source_target_pairs={{0,1},{1,2},{2,3},{3,4},{4,5},{5,6},{6,7},{8,9},{9,10},{10,11},{11... | collective-permute-start | bytes 1572872 | tf_op jit(solution)/shard_map/ppermute | solution.py:47
  232.1 8.0 collective-permute-start.11
  249.7 10.6 %collective-permute-start.12 = (bf16[512,512]{1,0:T(8,128)(2,1)}, bf16[512,512]{1,0:T(8,128)(2,1)S(1)}, u32[]{:S(2)}, u32[]{:S(2)}) collective-permute-start(bf16[512,512]{1,0:T(8,128)(2,1)} %fusion.999), channel_id=1, source_target_pairs={{0,1},{1,2},{2,3},{3,4},{4,5},{5,6},{6,7},{8,9},{9,10},{10,11},{11... | collective-permute-start | bytes 1572872 | tf_op jit(solution)/shard_map/ppermute | solution.py:47
  264.9 9.8 copy-start.7
  269.8 8.0 copy-start.16
  269.8 10.9 %collective-permute-start.13 = (bf16[512,512]{1,0:T(8,128)(2,1)}, bf16[512,512]{1,0:T(8,128)(2,1)S(1)}, u32[]{:S(2)}, u32[]{:S(2)}) collective-permute-start(bf16[512,512]{1,0:T(8,128)(2,1)} %fusion.996), channel_id=1, source_target_pairs={{0,1},{1,2},{2,3},{3,4},{4,5},{5,6},{6,7},{8,9},{9,10},{10,11},{11... | collective-permute-start | bytes 1572872 | tf_op jit(solution)/shard_map/ppermute | solution.py:47
  285.2 9.2 copy-start.10
  290.1 10.4 collective-permute-start.14
  305.0 9.4 copy-start.14
  309.9 7.6 copy-start.20
  309.9 10.6 %collective-permute-start.15 = (bf16[512,512]{1,0:T(8,128)(2,1)}, bf16[512,512]{1,0:T(8,128)(2,1)S(1)}, u32[]{:S(2)}, u32[]{:S(2)}) collective-permute-start(bf16[512,512]{1,0:T(8,128)(2,1)} %fusion.990), channel_id=1, source_target_pairs={{0,1},{1,2},{2,3},{3,4},{4,5},{5,6},{6,7},{8,9},{9,10},{10,11},{11... | collective-permute-start | bytes 1572872 | tf_op jit(solution)/shard_map/ppermute | solution.py:47
  325.1 9.4 copy-start.22
  329.9 7.6 copy-start.24
  329.9 10.6 %collective-permute-start.16 = (bf16[512,512]{1,0:T(8,128)(2,1)}, bf16[512,512]{1,0:T(8,128)(2,1)S(1)}, u32[]{:S(2)}, u32[]{:S(2)}) collective-permute-start(bf16[512,512]{1,0:T(8,128)(2,1)} %fusion.987), channel_id=1, source_target_pairs={{0,1},{1,2},{2,3},{3,4},{4,5},{5,6},{6,7},{8,9},{9,10},{10,11},{11... | collective-permute-start | bytes 1572872 | tf_op jit(solution)/shard_map/ppermute | solution.py:47
  345.2 9.6 copy-start.26
  350.0 7.8 copy-start.28
  350.0 10.6 %collective-permute-start.17 = (bf16[512,512]{1,0:T(8,128)(2,1)}, bf16[512,512]{1,0:T(8,128)(2,1)S(1)}, u32[]{:S(2)}, u32[]{:S(2)}) collective-permute-start(bf16[512,512]{1,0:T(8,128)(2,1)} %fusion.984), channel_id=1, source_target_pairs={{0,1},{1,2},{2,3},{3,4},{4,5},{5,6},{6,7},{8,9},{9,10},{10,11},{11... | collective-permute-start | bytes 1572872 | tf_op jit(solution)/shard_map/ppermute | solution.py:47
  365.2 9.4 copy-start.30
  370.1 10.6 %collective-permute-start.18 = (bf16[512,512]{1,0:T(8,128)(2,1)}, bf16[512,512]{1,0:T(8,128)(2,1)S(1)}, u32[]{:S(2)}, u32[]{:S(2)}) collective-permute-start(bf16[512,512]{1,0:T(8,128)(2,1)} %fusion.981), channel_id=1, source_target_pairs={{0,1},{1,2},{2,3},{3,4},{4,5},{5,6},{6,7},{8,9},{9,10},{10,11},{11... | collective-permute-start | bytes 1572872 | tf_op jit(solution)/shard_map/ppermute | solution.py:47
  385.2 9.4 copy-start.34
  390.1 7.6 copy-start.36
  390.1 10.6 %collective-permute-start.19 = (bf16[512,512]{1,0:T(8,128)(2,1)}, bf16[512,512]{1,0:T(8,128)(2,1)S(1)}, u32[]{:S(2)}, u32[]{:S(2)}) collective-permute-start(bf16[512,512]{1,0:T(8,128)(2,1)} %fusion.978), channel_id=1, source_target_pairs={{0,1},{1,2},{2,3},{3,4},{4,5},{5,6},{6,7},{8,9},{9,10},{10,11},{11... | collective-permute-start | bytes 1572872 | tf_op jit(solution)/shard_map/ppermute | solution.py:47
  405.3 9.4 copy-start.38
  410.2 10.6 %collective-permute-start.20 = (bf16[512,512]{1,0:T(8,128)(2,1)}, bf16[512,512]{1,0:T(8,128)(2,1)S(1)}, u32[]{:S(2)}, u32[]{:S(2)}) collective-permute-start(bf16[512,512]{1,0:T(8,128)(2,1)} %fusion.975), channel_id=1, source_target_pairs={{0,1},{1,2},{2,3},{3,4},{4,5},{5,6},{6,7},{8,9},{9,10},{10,11},{11... | collective-permute-start | bytes 1572872 | tf_op jit(solution)/shard_map/ppermute | solution.py:47
  425.4 9.6 copy-start.42
  430.2 7.8 copy-start.44
  430.2 10.6 %collective-permute-start.21 = (bf16[512,512]{1,0:T(8,128)(2,1)}, bf16[512,512]{1,0:T(8,128)(2,1)S(1)}, u32[]{:S(2)}, u32[]{:S(2)}) collective-permute-start(bf16[512,512]{1,0:T(8,128)(2,1)} %fusion.972), channel_id=1, source_target_pairs={{0,1},{1,2},{2,3},{3,4},{4,5},{5,6},{6,7},{8,9},{9,10},{10,11},{11... | collective-permute-start | bytes 1572872 | tf_op jit(solution)/shard_map/ppermute | solution.py:47
  458.8 30.7 %copy-start.2 = (f32[512,1280]{1,0:T(8,128)}, f32[512,1280]{1,0:T(8,128)S(1)}, u32[]{:S(2)}) copy-start(f32[512,1280]{1,0:T(8,128)S(1)} %fusion.657) | copy-start | bytes 7864324
  461.1 25.6 %copy-start.4 = (f32[512,1280]{1,0:T(8,128)}, f32[512,1280]{1,0:T(8,128)S(1)}, u32[]{:S(2)}) copy-start(f32[512,1280]{1,0:T(8,128)S(1)} %fusion.546) | copy-start | bytes 7864324
  462.9 11.5 %copy-start.52 = (bf16[1,1280,512]{2,1,0:T(8,128)(2,1)S(1)}, bf16[1,1280,512]{2,1,0:T(8,128)(2,1)}, u32[]{:S(2)}) copy-start(bf16[1,1280,512]{2,1,0:T(8,128)(2,1)} %param.9) | copy-start | bytes 3932164
  462.9 11.4 %collective-permute-start.22 = (bf16[512,512]{1,0:T(8,128)(2,1)S(1)}, bf16[512,512]{1,0:T(8,128)(2,1)S(1)}, u32[]{:S(2)}, u32[]{:S(2)}) collective-permute-start(bf16[512,512]{1,0:T(8,128)(2,1)S(1)} %fusion.1304), channel_id=1, source_target_pairs={{1,0},{2,1},{3,2},{4,3},{5,4},{6,5},{7,6},{9,8},{10,9},{11,10},{12... | collective-permute-start | bytes 1572872 | tf_op jit(solution)/shard_map/ppermute | solution.py:57
  474.4 8.5 copy-start.45
  484.4 10.5 %collective-permute-start.23 = (bf16[512,512]{1,0:T(8,128)(2,1)S(1)}, bf16[512,512]{1,0:T(8,128)(2,1)S(1)}, u32[]{:S(2)}, u32[]{:S(2)}) collective-permute-start(bf16[512,512]{1,0:T(8,128)(2,1)S(1)} %fusion.1303), channel_id=1, source_target_pairs={{1,0},{2,1},{3,2},{4,3},{5,4},{6,5},{7,6},{9,8},{10,9},{11,10},{12... | collective-permute-start | bytes 1572872 | tf_op jit(solution)/shard_map/ppermute | solution.py:57
  510.0 10.5 %collective-permute-start.24 = (bf16[512,512]{1,0:T(8,128)(2,1)S(1)}, bf16[512,512]{1,0:T(8,128)(2,1)S(1)}, u32[]{:S(2)}, u32[]{:S(2)}) collective-permute-start(bf16[512,512]{1,0:T(8,128)(2,1)S(1)} %fusion.1302), channel_id=1, source_target_pairs={{1,0},{2,1},{3,2},{4,3},{5,4},{6,5},{7,6},{9,8},{10,9},{11,10},{12... | collective-permute-start | bytes 1572872 | tf_op jit(solution)/shard_map/ppermute | solution.py:57
  535.6 10.5 %collective-permute-start.25 = (bf16[512,512]{1,0:T(8,128)(2,1)S(1)}, bf16[512,512]{1,0:T(8,128)(2,1)S(1)}, u32[]{:S(2)}, u32[]{:S(2)}) collective-permute-start(bf16[512,512]{1,0:T(8,128)(2,1)S(1)} %fusion.1301), channel_id=1, source_target_pairs={{1,0},{2,1},{3,2},{4,3},{5,4},{6,5},{7,6},{9,8},{10,9},{11,10},{12... | collective-permute-start | bytes 1572872 | tf_op jit(solution)/shard_map/ppermute | solution.py:57
  561.2 10.5 %collective-permute-start.26 = (bf16[512,512]{1,0:T(8,128)(2,1)S(1)}, bf16[512,512]{1,0:T(8,128)(2,1)S(1)}, u32[]{:S(2)}, u32[]{:S(2)}) collective-permute-start(bf16[512,512]{1,0:T(8,128)(2,1)S(1)} %fusion.1300), channel_id=1, source_target_pairs={{1,0},{2,1},{3,2},{4,3},{5,4},{6,5},{7,6},{9,8},{10,9},{11,10},{12... | collective-permute-start | bytes 1572872 | tf_op jit(solution)/shard_map/ppermute | solution.py:57
  586.8 10.5 %collective-permute-start.27 = (bf16[512,512]{1,0:T(8,128)(2,1)S(1)}, bf16[512,512]{1,0:T(8,128)(2,1)S(1)}, u32[]{:S(2)}, u32[]{:S(2)}) collective-permute-start(bf16[512,512]{1,0:T(8,128)(2,1)S(1)} %fusion.1299), channel_id=1, source_target_pairs={{1,0},{2,1},{3,2},{4,3},{5,4},{6,5},{7,6},{9,8},{10,9},{11,10},{12... | collective-permute-start | bytes 1572872 | tf_op jit(solution)/shard_map/ppermute | solution.py:57
  612.4 10.5 %collective-permute-start.28 = (bf16[512,512]{1,0:T(8,128)(2,1)S(1)}, bf16[512,512]{1,0:T(8,128)(2,1)S(1)}, u32[]{:S(2)}, u32[]{:S(2)}) collective-permute-start(bf16[512,512]{1,0:T(8,128)(2,1)S(1)} %fusion.1298), channel_id=1, source_target_pairs={{1,0},{2,1},{3,2},{4,3},{5,4},{6,5},{7,6},{9,8},{10,9},{11,10},{12... | collective-permute-start | bytes 1572872 | tf_op jit(solution)/shard_map/ppermute | solution.py:57
  638.0 10.5 %collective-permute-start.29 = (bf16[512,512]{1,0:T(8,128)(2,1)S(1)}, bf16[512,512]{1,0:T(8,128)(2,1)S(1)}, u32[]{:S(2)}, u32[]{:S(2)}) collective-permute-start(bf16[512,512]{1,0:T(8,128)(2,1)S(1)} %fusion.1297), channel_id=1, source_target_pairs={{1,0},{2,1},{3,2},{4,3},{5,4},{6,5},{7,6},{9,8},{10,9},{11,10},{12... | collective-permute-start | bytes 1572872 | tf_op jit(solution)/shard_map/ppermute | solution.py:57
  663.6 10.5 %collective-permute-start.30 = (bf16[512,512]{1,0:T(8,128)(2,1)S(1)}, bf16[512,512]{1,0:T(8,128)(2,1)S(1)}, u32[]{:S(2)}, u32[]{:S(2)}) collective-permute-start(bf16[512,512]{1,0:T(8,128)(2,1)S(1)} %fusion.1296), channel_id=1, source_target_pairs={{1,0},{2,1},{3,2},{4,3},{5,4},{6,5},{7,6},{9,8},{10,9},{11,10},{12... | collective-permute-start | bytes 1572872 | tf_op jit(solution)/shard_map/ppermute | solution.py:57
  689.2 10.5 %collective-permute-start.31 = (bf16[512,512]{1,0:T(8,128)(2,1)S(1)}, bf16[512,512]{1,0:T(8,128)(2,1)S(1)}, u32[]{:S(2)}, u32[]{:S(2)}) collective-permute-start(bf16[512,512]{1,0:T(8,128)(2,1)S(1)} %fusion.1295), channel_id=1, source_target_pairs={{1,0},{2,1},{3,2},{4,3},{5,4},{6,5},{7,6},{9,8},{10,9},{11,10},{12... | collective-permute-start | bytes 1572872 | tf_op jit(solution)/shard_map/ppermute | solution.py:57
  714.8 10.5 %collective-permute-start.32 = (bf16[512,512]{1,0:T(8,128)(2,1)S(1)}, bf16[512,512]{1,0:T(8,128)(2,1)S(1)}, u32[]{:S(2)}, u32[]{:S(2)}) collective-permute-start(bf16[512,512]{1,0:T(8,128)(2,1)S(1)} %fusion.1294), channel_id=1, source_target_pairs={{1,0},{2,1},{3,2},{4,3},{5,4},{6,5},{7,6},{9,8},{10,9},{11,10},{12... | collective-permute-start | bytes 1572872 | tf_op jit(solution)/shard_map/ppermute | solution.py:57
  740.4 10.5 %collective-permute-start.33 = (bf16[512,512]{1,0:T(8,128)(2,1)S(1)}, bf16[512,512]{1,0:T(8,128)(2,1)S(1)}, u32[]{:S(2)}, u32[]{:S(2)}) collective-permute-start(bf16[512,512]{1,0:T(8,128)(2,1)S(1)} %fusion.1293), channel_id=1, source_target_pairs={{1,0},{2,1},{3,2},{4,3},{5,4},{6,5},{7,6},{9,8},{10,9},{11,10},{12... | collective-permute-start | bytes 1572872 | tf_op jit(solution)/shard_map/ppermute | solution.py:57
  766.0 10.5 %collective-permute-start.34 = (bf16[512,512]{1,0:T(8,128)(2,1)S(1)}, bf16[512,512]{1,0:T(8,128)(2,1)S(1)}, u32[]{:S(2)}, u32[]{:S(2)}) collective-permute-start(bf16[512,512]{1,0:T(8,128)(2,1)S(1)} %fusion.1292), channel_id=1, source_target_pairs={{1,0},{2,1},{3,2},{4,3},{5,4},{6,5},{7,6},{9,8},{10,9},{11,10},{12... | collective-permute-start | bytes 1572872 | tf_op jit(solution)/shard_map/ppermute | solution.py:57
  791.6 10.5 %collective-permute-start.35 = (bf16[512,512]{1,0:T(8,128)(2,1)S(1)}, bf16[512,512]{1,0:T(8,128)(2,1)S(1)}, u32[]{:S(2)}, u32[]{:S(2)}) collective-permute-start(bf16[512,512]{1,0:T(8,128)(2,1)S(1)} %fusion.1291), channel_id=1, source_target_pairs={{1,0},{2,1},{3,2},{4,3},{5,4},{6,5},{7,6},{9,8},{10,9},{11,10},{12... | collective-permute-start | bytes 1572872 | tf_op jit(solution)/shard_map/ppermute | solution.py:57
  817.2 10.5 %collective-permute-start.36 = (bf16[512,512]{1,0:T(8,128)(2,1)S(1)}, bf16[512,512]{1,0:T(8,128)(2,1)S(1)}, u32[]{:S(2)}, u32[]{:S(2)}) collective-permute-start(bf16[512,512]{1,0:T(8,128)(2,1)S(1)} %fusion.1290), channel_id=1, source_target_pairs={{1,0},{2,1},{3,2},{4,3},{5,4},{6,5},{7,6},{9,8},{10,9},{11,10},{12... | collective-permute-start | bytes 1572872 | tf_op jit(solution)/shard_map/ppermute | solution.py:57
  842.8 10.5 %collective-permute-start.37 = (bf16[512,512]{1,0:T(8,128)(2,1)S(1)}, bf16[512,512]{1,0:T(8,128)(2,1)S(1)}, u32[]{:S(2)}, u32[]{:S(2)}) collective-permute-start(bf16[512,512]{1,0:T(8,128)(2,1)S(1)} %fusion.1289), channel_id=1, source_target_pairs={{1,0},{2,1},{3,2},{4,3},{5,4},{6,5},{7,6},{9,8},{10,9},{11,10},{12... | collective-permute-start | bytes 1572872 | tf_op jit(solution)/shard_map/ppermute | solution.py:57
  868.4 10.5 %collective-permute-start.38 = (bf16[512,512]{1,0:T(8,128)(2,1)S(1)}, bf16[512,512]{1,0:T(8,128)(2,1)S(1)}, u32[]{:S(2)}, u32[]{:S(2)}) collective-permute-start(bf16[512,512]{1,0:T(8,128)(2,1)S(1)} %fusion.1288), channel_id=1, source_target_pairs={{1,0},{2,1},{3,2},{4,3},{5,4},{6,5},{7,6},{9,8},{10,9},{11,10},{12... | collective-permute-start | bytes 1572872 | tf_op jit(solution)/shard_map/ppermute | solution.py:57
  894.0 10.5 %collective-permute-start.39 = (bf16[512,512]{1,0:T(8,128)(2,1)S(1)}, bf16[512,512]{1,0:T(8,128)(2,1)S(1)}, u32[]{:S(2)}, u32[]{:S(2)}) collective-permute-start(bf16[512,512]{1,0:T(8,128)(2,1)S(1)} %fusion.1287), channel_id=1, source_target_pairs={{1,0},{2,1},{3,2},{4,3},{5,4},{6,5},{7,6},{9,8},{10,9},{11,10},{12... | collective-permute-start | bytes 1572872 | tf_op jit(solution)/shard_map/ppermute | solution.py:57
  919.6 10.5 %collective-permute-start.40 = (bf16[512,512]{1,0:T(8,128)(2,1)S(1)}, bf16[512,512]{1,0:T(8,128)(2,1)S(1)}, u32[]{:S(2)}, u32[]{:S(2)}) collective-permute-start(bf16[512,512]{1,0:T(8,128)(2,1)S(1)} %fusion.1286), channel_id=1, source_target_pairs={{1,0},{2,1},{3,2},{4,3},{5,4},{6,5},{7,6},{9,8},{10,9},{11,10},{12... | collective-permute-start | bytes 1572872 | tf_op jit(solution)/shard_map/ppermute | solution.py:57
  945.2 10.5 %collective-permute-start.41 = (bf16[512,512]{1,0:T(8,128)(2,1)S(1)}, bf16[512,512]{1,0:T(8,128)(2,1)S(1)}, u32[]{:S(2)}, u32[]{:S(2)}) collective-permute-start(bf16[512,512]{1,0:T(8,128)(2,1)S(1)} %fusion.1285), channel_id=1, source_target_pairs={{1,0},{2,1},{3,2},{4,3},{5,4},{6,5},{7,6},{9,8},{10,9},{11,10},{12... | collective-permute-start | bytes 1572872 | tf_op jit(solution)/shard_map/ppermute | solution.py:57
  970.8 10.5 %collective-permute-start.42 = (bf16[512,512]{1,0:T(8,128)(2,1)S(1)}, bf16[512,512]{1,0:T(8,128)(2,1)S(1)}, u32[]{:S(2)}, u32[]{:S(2)}) collective-permute-start(bf16[512,512]{1,0:T(8,128)(2,1)S(1)} %fusion.1284), channel_id=1, source_target_pairs={{1,0},{2,1},{3,2},{4,3},{5,4},{6,5},{7,6},{9,8},{10,9},{11,10},{12... | collective-permute-start | bytes 1572872 | tf_op jit(solution)/shard_map/ppermute | solution.py:57
  996.4 10.5 %collective-permute-start.43 = (bf16[512,512]{1,0:T(8,128)(2,1)S(1)}, bf16[512,512]{1,0:T(8,128)(2,1)S(1)}, u32[]{:S(2)}, u32[]{:S(2)}) collective-permute-start(bf16[512,512]{1,0:T(8,128)(2,1)S(1)} %fusion.1283), channel_id=1, source_target_pairs={{1,0},{2,1},{3,2},{4,3},{5,4},{6,5},{7,6},{9,8},{10,9},{11,10},{12... | collective-permute-start | bytes 1572872 | tf_op jit(solution)/shard_map/ppermute | solution.py:57
  (36 other events, 96.2 us)
where the time goes:
time: 1060 us; the launch traced here: 1040 us
  matrix products  548 us (52%)
  waiting for transfers between devices  189 us (18%)
  starting transfers between devices  145 us (14%)
  other arithmetic  97.5 us (9%)
  local copies, waits for them, and re-layouts  54.9 us (5%)
    dot_general x90, matrix products, layer(): gate = jnp.dot(a, w['w_gate'], preferred_element_type=jnp.float32)  224 us
    dot_general x68, matrix products, matmul(): jnp.dot(a, w, preferred_element_type=jnp.float32).astype(jnp.bfloat16)  203 us
    ppermute x22, waiting for transfers between devices, step(): came = lax.ppermute(by_h, 'pp', back_again)  125 us
    dot_general x68, matrix products, layer(): up = jnp.dot(a, w['w_up'], preferred_element_type=jnp.float32)  120 us
    ppermute x22, starting transfers between devices, step(): came = lax.ppermute(stage(weights, h), 'pp', onward)  96 us
    ppermute x22, waiting for transfers between devices, step(): came = lax.ppermute(stage(weights, h), 'pp', onward)  64.5 us
    ppermute x22, starting transfers between devices, step(): came = lax.ppermute(by_h, 'pp', back_again)  49.4 us
    dynamic_update_slice x23, other arithmetic, step(): lax.dynamic_update_index_in_dim(kept, jnp.where(at_work, h, was), number, 0)  34.3 us
  transfers between devices with their start and end apart: 44, of which 41 were waited for; matrix products, arithmetic and copies ran while one was open for 12% of the time, Pallas kernels for 0%

commit v1 on v0

v1 whole, which is shorter than its diff:
```python
import functools

import jax
import jax.numpy as jnp
from jax import lax
from jax.experimental import pallas as pl
from jax.experimental.pallas import tpu as pltpu
from jax.sharding import PartitionSpec as P

f32, bf16 = jnp.float32, jnp.bfloat16
MESH = pl.DeviceIdType.MESH
PARTS = 2
RING_F, RING_B = 4, 2
SENDS = 4
LATE = 3
STAGES = 8


def ahead_of(me):
    return (3 * (STAGES - 1 - me)) // 2


def late_of(me):
    return jnp.clip(me - 4, 0, LATE)


def dot(a, b):
    return jnp.dot(a, b, preferred_element_type=f32)


def dot_t(a, b):
    return lax.dot_general(a, b, (((1,), (1,)), ((), ())), preferred_element_type=f32)


def scale_of(wide):
    return lax.rsqrt(jnp.mean(wide * wide, -1, keepdims=True) + 1e-6)


def kernel(
    x, dy, w_gate, w_up, w_down, by_gate, by_up, by_down, spill,
    wg, wu, wd, hs, ds, ring, ps, dgs, dus, a_t, dy_t, out_f, out_b, sum_g, sum_u, sum_d,
    w_sem, f_recv, b_recv, f_send, b_send, spill_sem, fetch_sem, end_sem,
):
    micro, tokens, d = hs.shape
    ff = wg.shape[1]
    wide_block = 256 if ff % 256 == 0 else 128
    rows_n = tokens // PARTS
    chunks = micro * PARTS
    me = lax.axis_index("pp")
    first, last = me == 0, me == STAGES - 1
    ahead, late = ahead_of(me), late_of(me)
    resident = 2 * ahead + 1 <= RING_F + RING_B

    def rows_of(c):
        return pl.ds(c * rows_n, rows_n)

    def weights_in():
        return [
            pltpu.make_async_copy(src.at[0], dst, w_sem.at[i])
            for i, (src, dst) in enumerate(((w_gate, wg), (w_up, wu), (w_down, wd)))
        ]

    def load_x(t, c):
        return pltpu.make_async_copy(x.at[t, rows_of(c)], hs.at[t, rows_of(c)], f_recv.at[t * PARTS + c])

    def load_dy(t, c):
        return pltpu.make_async_copy(dy.at[t, rows_of(c)], ds.at[t, rows_of(c)], b_recv.at[t * PARTS + c])

    def onward(t, c):
        i = t * PARTS + c
        return pltpu.make_async_remote_copy(
            src_ref=out_f.at[i % SENDS],
            dst_ref=hs.at[t, rows_of(c)],
            send_sem=f_send.at[i % SENDS],
            recv_sem=f_recv.at[i],
            device_id={"pp": me + 1},
            device_id_type=MESH,
        )

    def back_again(t, c):
        i = t * PARTS + c
        return pltpu.make_async_remote_copy(
            src_ref=out_b.at[i % SENDS],
            dst_ref=ds.at[t, rows_of(c)],
            send_sem=b_send.at[i % SENDS],
            recv_sem=b_recv.at[i],
            device_id={"pp": me - 1},
            device_id_type=MESH,
        )

    def put_away(i):
        return pltpu.make_async_copy(ring.at[i % RING_F], spill.at[i], spill_sem.at[i % RING_F])

    def fetch(i):
        return pltpu.make_async_copy(spill.at[i], ring.at[RING_F + i % RING_B], fetch_sem.at[i % RING_B])

    barrier = pltpu.get_barrier_semaphore()

    @pl.when(jnp.logical_not(last))
    def _():
        pl.semaphore_signal(barrier, inc=1, device_id={"pp": me + 1}, device_id_type=MESH)

    @pl.when(jnp.logical_not(first))
    def _():
        pl.semaphore_signal(barrier, inc=1, device_id={"pp": me - 1}, device_id_type=MESH)

    for copy in weights_in():
        copy.start()

    @pl.when(first)
    def _():
        @pl.loop(0, micro)
        def _(t):
            for c in range(PARTS):
                load_x(t, c).start()

    @pl.when(last)
    def _():
        @pl.loop(0, micro)
        def _(t):
            for c in range(PARTS):
                load_dy(t, c).start()

    for total in (sum_g, sum_u, sum_d):
        total[...] = jnp.zeros_like(total)
    for copy in weights_in():
        copy.wait()

    pl.semaphore_wait(barrier, jnp.where(first | last, 1, 2))

    def forward_math(t, c, slot, send):
        rows = rows_of(c)
        wide = hs[t, rows, :].astype(f32)
        a = (wide * scale_of(wide)).astype(bf16)
        products = []
        for n in range(ff // wide_block):
            cols = slice(n * wide_block, (n + 1) * wide_block)
            gate, up = dot(a, wg[:, cols]), dot(a, wu[:, cols])
            ring[slot, 0, :, cols] = gate
            ring[slot, 1, :, cols] = up
            if send:
                products.append((gate * jax.nn.sigmoid(gate) * up).astype(bf16))
        if send:
            y = dot(jnp.concatenate(products, -1), wd[...]).astype(bf16)
            out_f[(t * PARTS + c) % SENDS] = (wide + y.astype(f32)).astype(bf16)

    def forward(t, c):
        i = t * PARTS + c

        @pl.when(first)
        def _():
            load_x(t, c).wait()

        @pl.when(jnp.logical_not(first))
        def _():
            onward(t, c).wait_recv()

        @pl.when(jnp.logical_not(resident) & (i >= RING_F))
        def _():
            put_away(i - RING_F).wait()

        slot = jnp.where(resident, i % (RING_F + RING_B), i % RING_F)

        @pl.when(last)
        def _():
            forward_math(t, c, slot, False)

        @pl.when(jnp.logical_not(last))
        def _():
            @pl.when(i >= SENDS)
            def _():
                back = i - SENDS
                onward(back // PARTS, back % PARTS).wait_send()

            forward_math(t, c, slot, True)
            onward(t, c).start()

        @pl.when(jnp.logical_not(resident))
        def _():
            put_away(i).start()

    def backward_math(t, c, slot, send):
        rows = rows_of(c)
        at = t % (LATE + 1)
        by_y = ds[t, rows, :]
        for n in range(ff // wide_block):
            cols = slice(n * wide_block, (n + 1) * wide_block)
            by_product = dot_t(by_y, wd[cols, :]).astype(bf16).astype(f32)
            gate, up = ring[slot, 0, :, cols], ring[slot, 1, :, cols]
            sig = jax.nn.sigmoid(gate)
            silu = gate * sig
            ps[at, rows, cols] = (silu * up).astype(bf16)
            dus[at, rows, cols] = (by_product * silu).astype(bf16)
            dgs[at, rows, cols] = (by_product * up * (sig * (1.0 + gate * (1.0 - sig)))).astype(bf16)
        if send:
            by_a = (
                dot_t(dgs[at, rows, :], wg[...]).astype(bf16).astype(f32)
                + dot_t(dus[at, rows, :], wu[...]).astype(bf16).astype(f32)
            ).astype(bf16).astype(f32)
            wide = hs[t, rows, :].astype(f32)
            scale = scale_of(wide)
            pull = jnp.sum(by_a * wide, -1, keepdims=True) * (scale * scale * scale) * (-1.0 / d)
            by_h = (by_a * scale + wide * pull).astype(bf16)
            out_b[(t * PARTS + c) % SENDS] = (by_y.astype(f32) + by_h.astype(f32)).astype(bf16)

    def backward(t, c):
        i = t * PARTS + c

        @pl.when(last)
        def _():
            load_dy(t, c).wait()

        @pl.when(jnp.logical_not(last))
        def _():
            back_again(t, c).wait_recv()

        @pl.when(jnp.logical_not(resident))
        def _():
            fetch(i).wait()

            @pl.when(i + 1 < chunks)
            def _():
                fetch(i + 1).start()

        slot = jnp.where(resident, i % (RING_F + RING_B), RING_F + i % RING_B)

        @pl.when(first)
        def _():
            backward_math(t, c, slot, False)

        @pl.when(jnp.logical_not(first))
        def _():
            @pl.when(i >= SENDS)
            def _():
                back = i - SENDS
                back_again(back // PARTS, back % PARTS).wait_send()

            backward_math(t, c, slot, True)
            back_again(t, c).start()

    def by_weights(t):
        at = t % (LATE + 1)
        wide = hs[t].astype(f32)
        a_t[...] = (wide * scale_of(wide)).astype(bf16).T
        dy_t[...] = ds[t].T
        for total, left, right in ((sum_d, dy_t, ps), (sum_g, a_t, dgs), (sum_u, a_t, dus)):
            for n in range(ff // wide_block):
                cols = slice(n * wide_block, (n + 1) * wide_block)
                total[:, cols] += dot(left[...], right[at, :, cols]).astype(bf16).astype(f32)

    @pl.loop(0, micro + max(ahead_of(k) + max(0, min(k - 4, LATE)) for k in range(STAGES)))
    def _(t):
        u = t - ahead
        v = u - late

        @pl.when(jnp.logical_not(resident) & (t == micro))
        def _():
            for i in range(chunks - RING_F, chunks):
                put_away(i).wait()

        for c in range(PARTS):

            @pl.when(t < micro)
            def _(c=c):
                forward(t, c)

            @pl.when((u >= 0) & (u < micro))
            def _(c=c):
                backward(u, c)

        @pl.when(jnp.logical_not(resident) & (u == -1))
        def _():
            fetch(0).start()

        @pl.when((v >= 0) & (v < micro))
        def _():
            by_weights(v)

    copies = []
    for i, (total, to, out) in enumerate(((sum_g, dgs, by_gate), (sum_u, dus, by_up), (sum_d, ps, by_down))):
        to[0] = total[...].astype(bf16)
        copies.append(pltpu.make_async_copy(to.at[0], out.at[0], end_sem.at[i]))
        copies[-1].start()

    @pl.when(jnp.logical_not(last))
    def _():
        for i in range(chunks - SENDS, chunks):
            onward(i // PARTS, i % PARTS).wait_send()

    @pl.when(jnp.logical_not(first))
    def _():
        for i in range(chunks - SENDS, chunks):
            back_again(i // PARTS, i % PARTS).wait_send()

    for copy in copies:
        copy.wait()


def solution(mesh):
    def step(x, dy, w_gate, w_up, w_down):
        micro, tokens, d = x.shape
        ff = w_gate.shape[2]
        rows, chunks = tokens // PARTS, micro * PARTS
        flops = 9 * micro * 2 * tokens * d * ff
        anywhere = pl.BlockSpec(memory_space=pl.ANY)
        by_gate, by_up, by_down, _ = pl.pallas_call(
            kernel,
            out_shape=[jax.ShapeDtypeStruct((1, d, ff), bf16)] * 3
            + [jax.ShapeDtypeStruct((chunks, 2, rows, ff), f32)],
            in_specs=[anywhere] * 5,
            out_specs=[anywhere] * 4,
            scratch_shapes=[
                pltpu.VMEM((d, ff), bf16),
                pltpu.VMEM((d, ff), bf16),
                pltpu.VMEM((ff, d), bf16),
                pltpu.VMEM((micro, tokens, d), bf16),
                pltpu.VMEM((micro, tokens, d), bf16),
                pltpu.VMEM((RING_F + RING_B, 2, rows, ff), f32),
                *[pltpu.VMEM((LATE + 1, tokens, ff), bf16)] * 3,
                pltpu.VMEM((d, tokens), bf16),
                pltpu.VMEM((d, tokens), bf16),
                pltpu.VMEM((SENDS, rows, d), bf16),
                pltpu.VMEM((SENDS, rows, d), bf16),
                *[pltpu.VMEM((d, ff), f32)] * 3,
                pltpu.SemaphoreType.DMA((3,)),
                pltpu.SemaphoreType.DMA((chunks,)),
                pltpu.SemaphoreType.DMA((chunks,)),
                pltpu.SemaphoreType.DMA((SENDS,)),
                pltpu.SemaphoreType.DMA((SENDS,)),
                pltpu.SemaphoreType.DMA((RING_F,)),
                pltpu.SemaphoreType.DMA((RING_B,)),
                pltpu.SemaphoreType.DMA((3,)),
            ],
            compiler_params=pltpu.CompilerParams(
                collective_id=0, has_side_effects=True, vmem_limit_bytes=67043328
            ),
            cost_estimate=pl.CostEstimate(flops=flops, bytes_accessed=0, transcendentals=0),
            name="stage",
        )(x, dy, w_gate, w_up, w_down)
        return by_gate, by_up, jnp.swapaxes(by_down, 1, 2)

    return jax.shard_map(
        step,
        mesh=mesh,
        in_specs=(P("rep", None, None),) * 2 + (P("pp", None, None),) * 3,
        out_specs=(P(("rep", "pp"), None, None),) * 3,
        check_vma=False,
    )
```

time: 1060 us -> 199 us (0.19)
  the two profiles are of different devices: /device:TPU:13 before, /device:TPU:0 now
where the time goes in v1:
time: 199 us
  Pallas kernels  193 us (97%)
  local copies, waits for them, and re-layouts  5.38 us (3%)
    pallas_call x1, Pallas kernels, step(): pl.pallas_call(kernel, out_shape=[jax.ShapeDtypeStruct((1, d, ff), bf16)]...  193 us
    unnamed x7, local copies, waits for them, and re-layouts  5.38 us

profile of v1, /device:TPU:0, one launch (start us, length us, event | category | flops | bytes accessed | tf_op | source)
XLA Modules:
  0.0 198.8 jit_solution(12186183313390333001)
XLA Ops:
  0.6 192.8 %stage.1 = (bf16[1,512,1280]{2,1,0:T(8,128)(2,1)}, bf16[1,512,1280]{2,1,0:T(8,128)(2,1)}, bf16[1,512,1280]{2,1,0:T(8,128)(2,1)}, f32[32,2,256,1280]{3,2,1,0:T(8,128)}) custom-call(bf16[16,512,512]{2,1,0:T(8,128)(2,1)} %x.1, bf16[16,512,512]{2,1,0:T(8,128)(2,1)} %dy.1, bf16[1,512,1280]{2,1,0:T(8,128)(2,1)} %w_gate.1, bf16[1,512,1280]{2,1,0:T(8,128)(2,1)} %w_up.1, ...), custom_call_target="tpu_custom_call" | custom-call | flops 96636764160 | tf_op jit(solution)/shard_map/stage/pallas_call | solution.py:306
  193.4 0.0 copy-start.1
  193.4 2.5 %copy.8 = bf16[1,1280,512]{2,1,0:T(8,128)(2,1)} copy(bf16[1,1280,512]{1,2,0:T(8,128)(2,1)} %bitcast.1) | data formatting | bytes 2621440
  196.0 0.0 copy-done.1
  196.0 0.0 copy-start
  196.0 1.1 copy.11
  197.0 0.7 copy-done
  197.8 1.1 copy.12
Async XLA Ops:
  193.4 2.5 %copy-start.1 = (bf16[1,512,1280]{2,1,0:T(8,128)(2,1)S(1)}, bf16[1,512,1280]{2,1,0:T(8,128)(2,1)}, u32[]{:S(2)}) copy-start(bf16[1,512,1280]{2,1,0:T(8,128)(2,1)} %get-tuple-element.15) | copy-start | bytes 3932164
  196.0 1.8 copy-start

commit v2 on v1

--- a/solution.py
+++ b/solution.py
@@ -12,16 +12,17 @@
 PARTS = 2
 RING_F, RING_B = 4, 2
 SENDS = 4
-LATE = 3
+KEPT = 4
 STAGES = 8
 
 
 def ahead_of(me):
-    return (3 * (STAGES - 1 - me)) // 2
+    behind = STAGES - 1 - me
+    return 2 * behind - behind % 2
 
 
 def late_of(me):
-    return jnp.clip(me - 4, 0, LATE)
+    return 2 * me
 
 
 def dot(a, b):
@@ -37,9 +38,9 @@
 
 
 def kernel(
-    x, dy, w_gate, w_up, w_down, by_gate, by_up, by_down, spill,
-    wg, wu, wd, hs, ds, ring, ps, dgs, dus, a_t, dy_t, out_f, out_b, sum_g, sum_u, sum_d,
-    w_sem, f_recv, b_recv, f_send, b_send, spill_sem, fetch_sem, end_sem,
+    x, dy, w_gate, w_up, w_down, by_gate, by_up, by_down, spill, shelf,
+    wg, wu, wd, hs, ds, ring, kept, a_t, dy_t, out_f, out_b, sum_g, sum_u, sum_d,
+    w_sem, f_recv, b_recv, f_send, b_send, spill_sem, fetch_sem, shelf_sem, unshelf_sem, end_sem,
 ):
     micro, tokens, d = hs.shape
     ff = wg.shape[1]
@@ -50,6 +51,8 @@
     first, last = me == 0, me == STAGES - 1
     ahead, late = ahead_of(me), late_of(me)
     resident = 2 * ahead + 1 <= RING_F + RING_B
+    at_once = late < KEPT
+    half = KEPT // 2
 
     def rows_of(c):
         return pl.ds(c * rows_n, rows_n)
@@ -93,6 +96,12 @@
 
     def fetch(i):
         return pltpu.make_async_copy(spill.at[i], ring.at[RING_F + i % RING_B], fetch_sem.at[i % RING_B])
+
+    def shelve(u):
+        return pltpu.make_async_copy(kept.at[u % half], shelf.at[u], shelf_sem.at[u % half])
+
+    def unshelve(v):
+        return pltpu.make_async_copy(shelf.at[v], kept.at[half + v % half], unshelf_sem.at[v % half])
 
     barrier = pltpu.get_barrier_semaphore()
 
@@ -181,7 +190,7 @@
 
     def backward_math(t, c, slot, send):
         rows = rows_of(c)
-        at = t % (LATE + 1)
+        at = jnp.where(at_once, t % KEPT, t % half)
         by_y = ds[t, rows, :]
         for n in range(ff // wide_block):
             cols = slice(n * wide_block, (n + 1) * wide_block)
@@ -189,13 +198,13 @@
             gate, up = ring[slot, 0, :, cols], ring[slot, 1, :, cols]
             sig = jax.nn.sigmoid(gate)
             silu = gate * sig
-            ps[at, rows, cols] = (silu * up).astype(bf16)
-            dus[at, rows, cols] = (by_product * silu).astype(bf16)
-            dgs[at, rows, cols] = (by_product * up * (sig * (1.0 + gate * (1.0 - sig)))).astype(bf16)
+            kept[at, 0, rows, cols] = (silu * up).astype(bf16)
+            kept[at, 2, rows, cols] = (by_product * silu).astype(bf16)
+            kept[at, 1, rows, cols] = (by_product * up * (sig * (1.0 + gate * (1.0 - sig)))).astype(bf16)
         if send:
             by_a = (
-                dot_t(dgs[at, rows, :], wg[...]).astype(bf16).astype(f32)
-                + dot_t(dus[at, rows, :], wu[...]).astype(bf16).astype(f32)
+                dot_t(kept[at, 1, rows, :], wg[...]).astype(bf16).astype(f32)
+                + dot_t(kept[at, 2, rows, :], wu[...]).astype(bf16).astype(f32)
             ).astype(bf16).astype(f32)
             wide = hs[t, rows, :].astype(f32)
             scale = scale_of(wide)
@@ -224,6 +233,12 @@
 
         slot = jnp.where(resident, i % (RING_F + RING_B), RING_F + i % RING_B)
 
+        if c == 0:
+
+            @pl.when(jnp.logical_not(at_once) & (t >= half))
+            def _():
+                shelve(t - half).wait()
+
         @pl.when(first)
         def _():
             backward_math(t, c, slot, False)
@@ -238,17 +253,32 @@
             backward_math(t, c, slot, True)
             back_again(t, c).start()
 
+        if c == PARTS - 1:
+
+            @pl.when(jnp.logical_not(at_once))
+            def _():
+                shelve(t).start()
+
     def by_weights(t):
-        at = t % (LATE + 1)
+        at = jnp.where(at_once, t % KEPT, half + t % half)
+
+        @pl.when(jnp.logical_not(at_once))
+        def _():
+            unshelve(t).wait()
+
+            @pl.when(t + 1 < micro)
+            def _():
+                unshelve(t + 1).start()
+
         wide = hs[t].astype(f32)
         a_t[...] = (wide * scale_of(wide)).astype(bf16).T
         dy_t[...] = ds[t].T
-        for total, left, right in ((sum_d, dy_t, ps), (sum_g, a_t, dgs), (sum_u, a_t, dus)):
+        for i, (total, left) in enumerate(((sum_d, dy_t), (sum_g, a_t), (sum_u, a_t))):
             for n in range(ff // wide_block):
                 cols = slice(n * wide_block, (n + 1) * wide_block)
-                total[:, cols] += dot(left[...], right[at, :, cols]).astype(bf16).astype(f32)
-
-    @pl.loop(0, micro + max(ahead_of(k) + max(0, min(k - 4, LATE)) for k in range(STAGES)))
+                total[:, cols] += dot(left[...], kept[at, i, :, cols]).astype(bf16).astype(f32)
+
+    @pl.loop(0, micro + max(ahead_of(k) + late_of(k) for k in range(STAGES)))
     def _(t):
         u = t - ahead
         v = u - late
@@ -258,6 +288,11 @@
             for i in range(chunks - RING_F, chunks):
                 put_away(i).wait()
 
+        @pl.when(jnp.logical_not(at_once) & (u == micro))
+        def _():
+            for i in range(micro - half, micro):
+                shelve(i).wait()
+
         for c in range(PARTS):
 
             @pl.when(t < micro)
@@ -272,14 +307,18 @@
         def _():
             fetch(0).start()
 
+        @pl.when(jnp.logical_not(at_once) & (v == -1))
+        def _():
+            unshelve(0).start()
+
         @pl.when((v >= 0) & (v < micro))
         def _():
             by_weights(v)
 
     copies = []
-    for i, (total, to, out) in enumerate(((sum_g, dgs, by_gate), (sum_u, dus, by_up), (sum_d, ps, by_down))):
-        to[0] = total[...].astype(bf16)
-        copies.append(pltpu.make_async_copy(to.at[0], out.at[0], end_sem.at[i]))
+    for i, (total, out) in enumerate(((sum_g, by_gate), (sum_u, by_up), (sum_d, by_down))):
+        kept[0, i] = total[...].astype(bf16)
+        copies.append(pltpu.make_async_copy(kept.at[0, i], out.at[0], end_sem.at[i]))
         copies[-1].start()
 
     @pl.when(jnp.logical_not(last))
@@ -303,12 +342,12 @@
         rows, chunks = tokens // PARTS, micro * PARTS
         flops = 9 * micro * 2 * tokens * d * ff
         anywhere = pl.BlockSpec(memory_space=pl.ANY)
-        by_gate, by_up, by_down, _ = pl.pallas_call(
+        by_gate, by_up, by_down, *_ = pl.pallas_call(
             kernel,
             out_shape=[jax.ShapeDtypeStruct((1, d, ff), bf16)] * 3
-            + [jax.ShapeDtypeStruct((chunks, 2, rows, ff), f32)],
+            + [jax.ShapeDtypeStruct((chunks, 2, rows, ff), f32), jax.ShapeDtypeStruct((micro, 3, tokens, ff), bf16)],
             in_specs=[anywhere] * 5,
-            out_specs=[anywhere] * 4,
+            out_specs=[anywhere] * 5,
             scratch_shapes=[
                 pltpu.VMEM((d, ff), bf16),
                 pltpu.VMEM((d, ff), bf16),
@@ -316,7 +355,7 @@
                 pltpu.VMEM((micro, tokens, d), bf16),
                 pltpu.VMEM((micro, tokens, d), bf16),
                 pltpu.VMEM((RING_F + RING_B, 2, rows, ff), f32),
-                *[pltpu.VMEM((LATE + 1, tokens, ff), bf16)] * 3,
+                pltpu.VMEM((KEPT, 3, tokens, ff), bf16),
                 pltpu.VMEM((d, tokens), bf16),
                 pltpu.VMEM((d, tokens), bf16),
                 pltpu.VMEM((SENDS, rows, d), bf16),
@@ -329,6 +368,8 @@
                 pltpu.SemaphoreType.DMA((SENDS,)),
                 pltpu.SemaphoreType.DMA((RING_F,)),
                 pltpu.SemaphoreType.DMA((RING_B,)),
+                pltpu.SemaphoreType.DMA((KEPT // 2,)),
+                pltpu.SemaphoreType.DMA((KEPT // 2,)),
                 pltpu.SemaphoreType.DMA((3,)),
             ],
             compiler_params=pltpu.CompilerParams(

time: 199 us -> 189 us (0.950)
  the two profiles are of different devices: /device:TPU:0 before, /device:TPU:13 now
where the time goes in v2:
time: 189 us; the launch traced here: 188 us
  Pallas kernels  182 us (96%)
  local copies, waits for them, and re-layouts  5.38 us (3%)
    pallas_call x1, Pallas kernels, step(): pl.pallas_call(kernel, out_shape=[jax.ShapeDtypeStruct((1, d, ff), bf16)]...  182 us
    unnamed x7, local copies, waits for them, and re-layouts  5.38 us

profile of v2, /device:TPU:13, one launch (start us, length us, event | category | flops | bytes accessed | tf_op | source)
XLA Modules:
  0.0 187.8 jit_solution(5625827362412686288)
XLA Ops:
  0.6 181.8 %stage.1 = (bf16[1,512,1280]{2,1,0:T(8,128)(2,1)}, bf16[1,512,1280]{2,1,0:T(8,128)(2,1)}, bf16[1,512,1280]{2,1,0:T(8,128)(2,1)}, f32[32,2,256,1280]{3,2,1,0:T(8,128)}, bf16[16,3,512,1280]{3,2,1,0:T(8,128)(2,1)}) custom-call(bf16[16,512,512]{2,1,0:T(8,128)(2,1)} %x.1, bf16[16,512,512]{2,1,0:T(8,128)(2,1)} %dy.1, bf16[1,512,1280]{2,1,0:T(8,128)(2,1)} %w_gate.1, ...), custom_call_target="tpu_custom_call" | custom-call | flops 96636764160 | tf_op jit(solution)/shard_map/stage/pallas_call | solution.py:345
  182.4 0.0 copy-start.1
  182.4 2.5 %copy.8 = bf16[1,1280,512]{2,1,0:T(8,128)(2,1)} copy(bf16[1,1280,512]{1,2,0:T(8,128)(2,1)} %bitcast.1) | data formatting | bytes 2621440
  184.9 0.0 copy-done.1
  185.0 0.0 copy-start
  185.0 1.1 copy.11
  186.0 0.7 copy-done
  186.7 1.1 copy.12
Async XLA Ops:
  182.4 2.5 %copy-start.1 = (bf16[1,512,1280]{2,1,0:T(8,128)(2,1)S(1)}, bf16[1,512,1280]{2,1,0:T(8,128)(2,1)}, u32[]{:S(2)}) copy-start(bf16[1,512,1280]{2,1,0:T(8,128)(2,1)} %get-tuple-element.15) | copy-start | bytes 3932164
  185.0 1.8 copy-start

commit v3 on v2

--- a/solution.py
+++ b/solution.py
@@ -22,7 +22,7 @@
 
 
 def late_of(me):
-    return 2 * me
+    return lax.min((5 * me + 2) // 2, 15)
 
 
 def dot(a, b):
@@ -130,8 +130,14 @@
             for c in range(PARTS):
                 load_dy(t, c).start()
 
-    for total in (sum_g, sum_u, sum_d):
-        total[...] = jnp.zeros_like(total)
+    def clear():
+        for total in (sum_g, sum_u, sum_d):
+            total[...] = jnp.zeros_like(total)
+
+    @pl.when(jnp.logical_not(first))
+    def _():
+        clear()
+
     for copy in weights_in():
         copy.wait()
 
@@ -278,7 +284,7 @@
                 cols = slice(n * wide_block, (n + 1) * wide_block)
                 total[:, cols] += dot(left[...], kept[at, i, :, cols]).astype(bf16).astype(f32)
 
-    @pl.loop(0, micro + max(ahead_of(k) + late_of(k) for k in range(STAGES)))
+    @pl.loop(0, micro + max(ahead_of(k) + min((5 * k + 2) // 2, 15) for k in range(STAGES)))
     def _(t):
         u = t - ahead
         v = u - late
@@ -287,6 +293,10 @@
         def _():
             for i in range(chunks - RING_F, chunks):
                 put_away(i).wait()
+
+        @pl.when(first & (t == 4))
+        def _():
+            clear()
 
         @pl.when(jnp.logical_not(at_once) & (u == micro))
         def _():
@@ -333,6 +343,12 @@
 
     for copy in copies:
         copy.wait()
+
+
+def hand_out(g, u, d, by_gate, by_up, by_down):
+    by_gate[...] = g[...]
+    by_up[...] = u[...]
+    by_down[0] = d[0].T
 
 
 def solution(mesh):
@@ -378,7 +394,15 @@
             cost_estimate=pl.CostEstimate(flops=flops, bytes_accessed=0, transcendentals=0),
             name="stage",
         )(x, dy, w_gate, w_up, w_down)
-        return by_gate, by_up, jnp.swapaxes(by_down, 1, 2)
+        across = pl.BlockSpec((1, d, 256), lambda i: (0, 0, i))
+        return pl.pallas_call(
+            hand_out,
+            grid=(ff // 256,),
+            out_shape=[jax.ShapeDtypeStruct((1, d, ff), bf16)] * 2 + [jax.ShapeDtypeStruct((1, ff, d), bf16)],
+            in_specs=[across] * 3,
+            out_specs=[across] * 2 + [pl.BlockSpec((1, 256, d), lambda i: (0, i, 0))],
+            name="hand_out",
+        )(by_gate, by_up, by_down)
 
     return jax.shard_map(
         step,

time: 189 us -> 188 us (level)
  local copies, waits for them, and re-layouts: 5.38 us -> 0 us
  Pallas kernels: 182 us -> 187 us
    pallas_call x0 -> x1, Pallas kernels: none -> 5.64 us  [step(): pl.pallas_call(hand_out, grid=(ff // 256,), out_shape=[jax.ShapeDtypeStru...]
    unnamed x7 -> x0, local copies, waits for them, and re-layouts: 5.38 us -> none
where the time goes in v3:
time: 188 us
  Pallas kernels  187 us (99%)
    pallas_call x1, Pallas kernels, step(): pl.pallas_call(kernel, out_shape=[jax.ShapeDtypeStruct((1, d, ff), bf16)]...  181 us
    pallas_call x1, Pallas kernels, step(): pl.pallas_call(hand_out, grid=(ff // 256,), out_shape=[jax.ShapeDtypeStru...  5.64 us

profile of v3, /device:TPU:13, one launch (start us, length us, event | category | flops | bytes accessed | tf_op | source)
XLA Modules:
  0.0 187.7 jit_solution(4520304306451929418)
XLA Ops:
  0.6 181.4 %stage.1 = (bf16[1,512,1280]{2,1,0:T(8,128)(2,1)}, bf16[1,512,1280]{2,1,0:T(8,128)(2,1)}, bf16[1,512,1280]{2,1,0:T(8,128)(2,1)}, f32[32,2,256,1280]{3,2,1,0:T(8,128)}, bf16[16,3,512,1280]{3,2,1,0:T(8,128)(2,1)}) custom-call(bf16[16,512,512]{2,1,0:T(8,128)(2,1)} %x.1, bf16[16,512,512]{2,1,0:T(8,128)(2,1)} %dy.1, bf16[1,512,1280]{2,1,0:T(8,128)(2,1)} %w_gate.1, ...), custom_call_target="tpu_custom_call" | custom-call | flops 96636764160 | tf_op jit(solution)/shard_map/stage/pallas_call | solution.py:361
  182.1 5.6 %hand_out.1 = (bf16[1,512,1280]{2,1,0:T(8,128)(2,1)}, bf16[1,512,1280]{2,1,0:T(8,128)(2,1)}, bf16[1,1280,512]{2,1,0:T(8,128)(2,1)}) custom-call(bf16[1,512,1280]{2,1,0:T(8,128)(2,1)} %get-tuple-element.6.g, bf16[1,512,1280]{2,1,0:T(8,128)(2,1)} %get-tuple-element.7.u, bf16[1,512,1280]{2,1,0:T(8,128)(2,1)} %get-tuple-element.8.d), custom_call_target="tpu_custom_call" | custom-call | tf_op jit(solution)/shard_map/hand_out/pallas_call | solution.py:398

commit v4 on v3

--- a/solution.py
+++ b/solution.py
@@ -343,12 +343,6 @@
 
     for copy in copies:
         copy.wait()
-
-
-def hand_out(g, u, d, by_gate, by_up, by_down):
-    by_gate[...] = g[...]
-    by_up[...] = u[...]
-    by_down[0] = d[0].T
 
 
 def solution(mesh):
@@ -394,15 +388,7 @@
             cost_estimate=pl.CostEstimate(flops=flops, bytes_accessed=0, transcendentals=0),
             name="stage",
         )(x, dy, w_gate, w_up, w_down)
-        across = pl.BlockSpec((1, d, 256), lambda i: (0, 0, i))
-        return pl.pallas_call(
-            hand_out,
-            grid=(ff // 256,),
-            out_shape=[jax.ShapeDtypeStruct((1, d, ff), bf16)] * 2 + [jax.ShapeDtypeStruct((1, ff, d), bf16)],
-            in_specs=[across] * 3,
-            out_specs=[across] * 2 + [pl.BlockSpec((1, 256, d), lambda i: (0, i, 0))],
-            name="hand_out",
-        )(by_gate, by_up, by_down)
+        return by_gate, by_up, jnp.swapaxes(by_down, 1, 2)
 
     return jax.shard_map(
         step,

time: 188 us -> 188 us (level)
  Pallas kernels: 187 us -> 181 us
  local copies, waits for them, and re-layouts: 0 us -> 5.38 us
    pallas_call x1 -> x0, Pallas kernels: 5.64 us -> none  [step(): pl.pallas_call(hand_out, grid=(ff // 256,), out_shape=[jax.ShapeDtypeStru...]
    unnamed x0 -> x7, local copies, waits for them, and re-layouts: none -> 5.38 us
where the time goes in v4:
time: 188 us; the launch traced here: 187 us
  Pallas kernels  181 us (96%)
  local copies, waits for them, and re-layouts  5.38 us (3%)
    pallas_call x1, Pallas kernels, step(): pl.pallas_call(kernel, out_shape=[jax.ShapeDtypeStruct((1, d, ff), bf16)]...  181 us
    unnamed x7, local copies, waits for them, and re-layouts  5.38 us

profile of v4, /device:TPU:13, one launch (start us, length us, event | category | flops | bytes accessed | tf_op | source)
XLA Modules:
  0.0 187.5 jit_solution(18238799476939526151)
XLA Ops:
  0.6 181.4 %stage.1 = (bf16[1,512,1280]{2,1,0:T(8,128)(2,1)}, bf16[1,512,1280]{2,1,0:T(8,128)(2,1)}, bf16[1,512,1280]{2,1,0:T(8,128)(2,1)}, f32[32,2,256,1280]{3,2,1,0:T(8,128)}, bf16[16,3,512,1280]{3,2,1,0:T(8,128)(2,1)}) custom-call(bf16[16,512,512]{2,1,0:T(8,128)(2,1)} %x.1, bf16[16,512,512]{2,1,0:T(8,128)(2,1)} %dy.1, bf16[1,512,1280]{2,1,0:T(8,128)(2,1)} %w_gate.1, ...), custom_call_target="tpu_custom_call" | custom-call | flops 96636764160 | tf_op jit(solution)/shard_map/stage/pallas_call | solution.py:355
  182.1 0.0 copy-start.1
  182.1 2.5 %copy.8 = bf16[1,1280,512]{2,1,0:T(8,128)(2,1)} copy(bf16[1,1280,512]{1,2,0:T(8,128)(2,1)} %bitcast.1) | data formatting | bytes 2621440
  184.6 0.0 copy-done.1
  184.6 0.0 copy-start
  184.6 1.1 copy.11
  185.7 0.7 copy-done
  186.4 1.1 copy.12
Async XLA Ops:
  182.1 2.5 %copy-start.1 = (bf16[1,512,1280]{2,1,0:T(8,128)(2,1)S(1)}, bf16[1,512,1280]{2,1,0:T(8,128)(2,1)}, u32[]{:S(2)}) copy-start(bf16[1,512,1280]{2,1,0:T(8,128)(2,1)} %get-tuple-element.15) | copy-start | bytes 3932164
  184.6 1.8 copy-start
